TPU v7x, 32 devices: a whole 2x2x4 slice. The times are simulated.
32 devices in a mesh: section: 4 (over y, x), dp: 8 (over z, core).
Axes of the slice: x: 2, y: 2, z: 4, core: 2. Of those that a mesh axis runs over, the one named last changes fastest.
Arguments:
- hidden_in: bfloat16 [2, 4, 4, 128, 4096], P(None, 'section', None, 'dp'), may hold values from -6 to 6
- out_grad: bfloat16 [4, 128, 4096], P(None, 'dp'), may hold values from -6 to 6
- gate_probs: float32 [2, 4, 4, 128, 2], P(None, 'section', None, 'dp'), may hold values from 0.1 to 1
- expert_ids: int32 [2, 4, 4, 128, 2], P(None, 'section', None, 'dp'), may hold values from 0 to 7, all different within a row
- task_ids: int32 [4, 8], P(None, 'dp'), may hold values from 0 to 1
- task_embed: float32 [2, 256], replicated, may hold values from -5 to 5
- slot_embed: float32 [2, 4, 8, 256], P(None, 'section'), may hold values from -5 to 5
- gen_down: bfloat16 [256, 65536], P(None, 'dp'), may hold values from -0.0078125 to 0.0078125
- gen_up: bfloat16 [256, 65536], P(None, 'dp'), may hold values from -0.09375 to 0.09375
Outputs:
- d_hidden: bfloat16 [4, 4, 128, 4096], P('section', None, 'dp')
- d_gen_down: float32 [256, 65536], P(None, 'dp')
- d_gen_up: float32 [256, 65536], P(None, 'dp')
- d_task_embed: float32 [2, 256], replicated
- d_slot_embed: float32 [2, 4, 8, 256], P(None, 'section')
Inputs may be any that keep to these rules, and one draw needn't show every extreme that they name: `expert_ids`: the two experts of a token differ.
All inputs are finite; a program needn't handle non-finite values.
Results may differ from a plain program's by a relative error of at most 0.025.
Values may be sent and summed in bfloat16 or wider, within the bound.
A program may use at most 128 MiB of HBM per device.

v0:
```python
import functools

import jax
import jax.numpy as jnp
from jax import lax
from jax.experimental import pallas as pl
from jax.experimental.pallas import tpu as pltpu
from jax.sharding import PartitionSpec as P

eps = 1e-05
MESH = pl.DeviceIdType.MESH
nt = (((1,), (1,)), ((), ()))
tn = (((0,), (0,)), ((), ()))


def relay(
    sections, blocks, micro, chunk,
    hid, grad, cols, adapt,
    hid_out, xn_out, cot_out, low_out, glow_out,
    landed, made, wide, send_sem, recv_sem,
):
    me = lax.axis_index("section")
    below = lax.rem(me + sections - 1, sections)
    above = lax.rem(me + 1, sections)
    total = blocks * micro
    groups, _, rows, width = adapt.shape
    ranks = groups * rows
    spans = [pl.ds(at, chunk) for at in range(0, width, chunk)]

    barrier = pltpu.get_barrier_semaphore()
    for other in (below, above):
        pl.semaphore_signal(
            barrier, inc=1, device_id={"section": other}, device_id_type=MESH
        )
    pl.semaphore_wait(barrier, 2)

    def copy_of(item, slot):
        return pltpu.make_async_remote_copy(
            src_ref=made.at[item],
            dst_ref=landed.at[slot],
            send_sem=send_sem.at[item],
            recv_sem=recv_sem.at[slot],
            device_id={"section": below},
            device_id_type=MESH,
        )

    def step(item, carry):
        block = blocks - 1 - item // micro
        spot = block * micro + item % micro
        kind_a, kind_b = 2 * block, 2 * block + 1
        x = hid[spot].astype(jnp.float32)
        inv = lax.rsqrt(jnp.mean(x * x, axis=-1, keepdims=True) + eps)
        xn_out[spot] = (x * inv).astype(jnp.bfloat16)
        weights = cols[spot]
        low = jnp.zeros((x.shape[0], ranks), jnp.float32)
        for span in spans:
            low += lax.dot_general(
                xn_out[spot, :, span], adapt[:, kind_a, :, span].reshape(ranks, chunk), nt,
                preferred_element_type=jnp.float32,
            )
        low_out[spot] = (weights * low).astype(jnp.bfloat16)

        first = (me == sections - 1) & (item < micro)

        @pl.when(first)
        def _():
            landed[item] = grad[item % micro]

        @pl.when(jnp.logical_not(first))
        def _():
            copy_of(item, item).wait_recv()

        cot_out[spot] = landed[item]
        back = jnp.zeros((x.shape[0], ranks), jnp.float32)
        for span in spans:
            back += lax.dot_general(
                landed[item, :, span], adapt[:, kind_b, :, span].reshape(ranks, chunk), nt,
                preferred_element_type=jnp.float32,
            )
        glow = (weights * back).astype(jnp.bfloat16)
        glow_out[spot] = glow
        dots = jnp.zeros((x.shape[0], 1), jnp.float32)
        for span in spans:
            part = jnp.dot(
                glow, adapt[:, kind_a, :, span].reshape(ranks, chunk),
                preferred_element_type=jnp.float32,
            )
            wide[:, span] = part
            xf = hid[spot, :, span].astype(jnp.float32) * inv
            dots += jnp.sum(part * xf, axis=-1, keepdims=True)
        dots = dots * (1.0 / width)
        for span in spans:
            xf = hid[spot, :, span].astype(jnp.float32) * inv
            dx = landed[item, :, span].astype(jnp.float32) + inv * (wide[:, span] - xf * dots)
            made[item, :, span] = dx.astype(jnp.bfloat16)

        @pl.when(me > 0)
        def _():
            copy_of(item, item).start()

        @pl.when((me == 0) & (item < total - micro))
        def _():
            copy_of(item, item + micro).start()

        @pl.when(item >= total - micro)
        def _():
            hid_out[item % micro] = made[item]

        return carry

    lax.fori_loop(0, total, step, 0)

    def drain(item, carry):
        @pl.when((me > 0) | (item < total - micro))
        def _():
            copy_of(item, item).wait_send()

        return carry

    lax.fori_loop(0, total, drain, 0)


def on_device(
    hidden_in, out_grad, gate_probs, expert_ids, task_ids, task_embed, slot_embed, gen_down, gen_up
):
    sections, ways = lax.axis_size("section"), lax.axis_size("dp")
    section_id = lax.axis_index("section")
    blocks, _, micro, tok, width = hidden_in.shape
    tasks, cond_width = task_embed.shape
    experts = slot_embed.shape[2]
    combos = tasks * experts
    span = gen_down.shape[1]
    per = max(1, span // width)
    cuts = max(1, width // span)
    piece = span // per
    kinds = 2 * blocks
    total = blocks * micro

    slots = lax.all_gather(slot_embed[:, 0], "section", axis=0)
    pre_all = task_embed[None, None, :, None, :] + slots[:, :, None, :, :]
    sig_all = jax.nn.sigmoid(pre_all)
    cond_all = (pre_all * sig_all).reshape(-1, cond_width).astype(jnp.bfloat16)
    pre_own = task_embed[None, :, None, :] + slot_embed[:, 0][:, None, :, :]
    cond_own = jax.nn.silu(pre_own).reshape(-1, cond_width).astype(jnp.bfloat16)

    def made_from(gen):
        out = jnp.dot(cond_own, gen, preferred_element_type=jnp.float32).astype(jnp.bfloat16)
        out = out.reshape(blocks, combos, per, piece).transpose(0, 2, 1, 3)
        return out.reshape(blocks, per * combos, piece)

    shard = jnp.stack([made_from(gen_down), made_from(gen_up)], axis=1)
    shard = shard.reshape(1, kinds, per * combos, piece)
    adapt = lax.all_gather(shard, "dp", axis=0, tiled=True)
    if cuts > 1:
        adapt = adapt.reshape(ways // cuts, cuts, kinds, combos, piece).transpose(0, 2, 3, 1, 4)
        adapt = adapt.reshape(ways // cuts, kinds, combos, width)
    groups = adapt.shape[0]
    ranks = groups * per * combos

    hot = (expert_ids[:, 0][..., None] == jnp.arange(experts, dtype=jnp.int32)).astype(jnp.float32)
    per_expert = jnp.sum(gate_probs[:, 0][..., None] * hot, axis=3)
    task_hot = (task_ids == jnp.arange(tasks, dtype=jnp.int32)).astype(jnp.float32)
    table = task_hot[None, :, None, :, None] * per_expert[:, :, :, None, :]
    cols = jnp.tile(table.reshape(total, tok, combos), (1, 1, ranks // combos))

    whole = pl.BlockSpec(memory_space=pltpu.VMEM)
    bf = jnp.bfloat16
    hid_out, xn, cot, low, glow = pl.pallas_call(
        functools.partial(relay, sections, blocks, micro, min(width, 1024)),
        out_shape=(
            jax.ShapeDtypeStruct((micro, tok, width), bf),
            jax.ShapeDtypeStruct((total, tok, width), bf),
            jax.ShapeDtypeStruct((total, tok, width), bf),
            jax.ShapeDtypeStruct((total, tok, ranks), bf),
            jax.ShapeDtypeStruct((total, tok, ranks), bf),
        ),
        in_specs=[whole] * 4,
        out_specs=(whole,) * 5,
        scratch_shapes=[
            pltpu.VMEM((total, tok, width), bf),
            pltpu.VMEM((total, tok, width), bf),
            pltpu.VMEM((tok, width), jnp.float32),
            pltpu.SemaphoreType.DMA((total,)),
            pltpu.SemaphoreType.DMA((total,)),
        ],
        compiler_params=pltpu.CompilerParams(
            collective_id=1, has_side_effects=True, vmem_limit_bytes=40 << 20
        ),
        name="relay",
    )(hidden_in.reshape(total, tok, width), out_grad, cols, adapt)

    scale = 1.0 / (micro * tok * ways)

    def grads(left, right):
        out = lax.dot_general(
            left.reshape(-1, ranks), right.reshape(-1, width), tn,
            preferred_element_type=jnp.float32,
        )
        out = (out * scale).astype(bf)
        if cuts > 1:
            out = out.reshape(ways // cuts, combos, cuts, piece).transpose(0, 2, 1, 3)
        return out.reshape(ways, 1, per * combos, piece)

    reduced = []
    for block in range(blocks):
        at = slice(block * micro, (block + 1) * micro)
        pair = jnp.concatenate([grads(glow[at], xn[at]), grads(low[at], cot[at])], axis=1)
        reduced.append(lax.psum_scatter(pair, "dp", scatter_dimension=0, tiled=True))
    own = jnp.concatenate(reduced, axis=0)
    every = lax.all_gather(own, "section", axis=0, tiled=True)
    every = every.reshape(sections * blocks, 2, per, combos, piece)
    every = every.transpose(1, 0, 3, 2, 4).reshape(2, -1, span)
    part = jnp.zeros((), jnp.float32)
    d_gens = []
    for which, gen in ((0, gen_down), (1, gen_up)):
        d_gens.append(
            lax.dot_general(cond_all, every[which], tn, preferred_element_type=jnp.float32)
        )
        part = part + lax.dot_general(every[which], gen, nt, preferred_element_type=jnp.float32)
    d_pre = part.reshape(pre_all.shape) * sig_all * (1.0 + pre_all * (1.0 - sig_all))
    sums = jnp.concatenate(
        [
            jnp.sum(d_pre, axis=2).reshape(-1, cond_width),
            jnp.sum(d_pre, axis=(0, 1, 3)),
        ]
    )
    sums = jnp.sum(lax.all_gather(sums, "dp", axis=0), axis=0)
    d_task = sums[-tasks:]
    d_slot = lax.dynamic_slice_in_dim(
        sums, section_id * blocks * experts, blocks * experts
    ).reshape(blocks, 1, experts, cond_width)
    return (hid_out[None], d_gens[0], d_gens[1], d_task, d_slot)


def solution(mesh):
    placed = (
        P(None, "section", None, "dp", None),
        P(None, "dp", None),
        P(None, "section", None, "dp", None),
        P(None, "section", None, "dp", None),
        P(None, "dp"),
        P(),
        P(None, "section", None, None),
        P(None, "dp"),
        P(None, "dp"),
    )
    return jax.shard_map(
        on_device,
        mesh=mesh,
        in_specs=placed,
        out_specs=(
            P("section", None, "dp", None),
            P(None, "dp"),
            P(None, "dp"),
            P(),
            P(None, "section", None, None),
        ),
        check_vma=False,
    )
```

profile of v0, /device:TPU:0, one launch (start us, length us, event | category | flops | bytes accessed | tf_op | source)
XLA Modules:
  0.0 364.6 jit_solution(6554014306756747214)
XLA Ops:
  8.0 3.0 convolution_convert_fusion
  11.7 3.0 convolution_convert_fusion.1
  15.5 1.0 copy.69
  17.6 83.9 %all-gather.6.cloned.1.call-done.adapt = bf16[8,4,32,4096]{3,2,1,0:T(8,128)(2,1)} async-done(((bf16[1,4,32,4096]{3,2,1,0:T(8,128)(2,1)}), bf16[8,4,32,4096]{3,2,1,0:T(8,128)(2,1)}) %all-gather.6.cloned.1.call-update) | async-done | bytes 8388624 | tf_op jit(solution)/shard_map/all_gather | solution.py:153
  101.5 3.4 copy-done
  104.9 57.9 %relay.1 = (bf16[4,16,4096]{2,1,0:T(8,128)(2,1)S(1)}, bf16[8,16,4096]{2,1,0:T(8,128)(2,1)S(1)}, bf16[8,16,4096]{2,1,0:T(8,128)(2,1)S(1)}, bf16[8,16,256]{2,1,0:T(8,128)(2,1)S(1)}, bf16[8,16,256]{2,1,0:T(8,128)(2,1)S(1)}) custom-call(bf16[8,16,4096]{2,1,0:T(8,128)(2,1)S(1)} %bitcast.98, bf16[4,16,4096]{2,1,0:T(8,128)(2,1)S(1)} %copy-done.2, ...), custom_call_target="tpu_custom_call" | custom-call | tf_op jit(solution)/shard_map/relay/pallas_call | solution.py:168
  164.3 2.4 pad_maximum_fusion.1
  166.7 1.1 copy-done.4
  169.3 2.4 pad_maximum_fusion
  171.8 41.6 %reduce-scatter.5.cloned.1.call-done = bf16[1,2,32,4096]{3,2,1,0:T(8,128)(2,1)} async-done(((bf16[8,2,32,4096]{3,2,1,0:T(8,128)(2,1)}), bf16[1,2,32,4096]{3,2,1,0:T(8,128)(2,1)}) %reduce-scatter.5.cloned.1.call-update) | async-done | bytes 524304 | tf_op jit(solution)/shard_map/reduce_scatter | solution.py:208
  213.4 51.3 %reduce-scatter.3.cloned.1.call-done = bf16[1,2,32,4096]{3,2,1,0:T(8,128)(2,1)} async-done(((bf16[8,2,32,4096]{3,2,1,0:T(8,128)(2,1)}), bf16[1,2,32,4096]{3,2,1,0:T(8,128)(2,1)}) %reduce-scatter.3.cloned.1.call-update) | async-done | bytes 524304 | tf_op jit(solution)/shard_map/reduce_scatter | solution.py:208
  264.7 2.3 pad_maximum_fusion.3
  267.0 8.4 %all-gather = f32[8,1,8,256]{3,2,1,0:T(8,128)S(1)} all-gather(f32[2,1,8,256]{3,2,1,0:T(8,128)S(1)} %copy-done.7), channel_id=2, replica_groups=mesh['section'=4,'dp'=8] {'section'}, dimensions={0}, use_global_device_ids=true | all-gather | bytes 81920 | tf_op jit(solution)/shard_map/all_gather | solution.py:139
  275.4 42.8 %all-gather.8.cloned.1.call-done = bf16[8,2,32,4096]{3,2,1,0:T(8,128)(2,1)} async-done(((bf16[2,2,32,4096]{3,2,1,0:T(8,128)(2,1)}), bf16[8,2,32,4096]{3,2,1,0:T(8,128)(2,1)}) %all-gather.8.cloned.1.call-update) | async-done | bytes 4194320 | tf_op jit(solution)/shard_map/all_gather | solution.py:210
  318.2 2.5 fusion.24
  320.7 2.2 copy.75
  322.9 1.3 copy.77
  324.2 2.2 copy.74
  326.4 1.3 copy.76
  327.7 1.5 fusion.27
  329.9 1.6 convolution_add_fusion
  331.6 4.7 %fusion.26 = f32[256,8192]{1,0:T(8,128)} fusion(bf16[128,256]{1,0:T(8,128)(2,1)S(1)} %bitcast.114, bf16[128,8192]{1,0:T(8,128)(2,1)S(1)} %bitcast.101), kind=kOutput, calls=%fused_computation.49 | convolution fusion | flops 536870912 | bytes 10551296 | tf_op jit(solution)/shard_map/dot_general | solution.py:217
  336.3 4.7 %fusion.25 = f32[256,8192]{1,0:T(8,128)} fusion(bf16[128,256]{1,0:T(8,128)(2,1)S(1)} %bitcast.115, bf16[128,8192]{1,0:T(8,128)(2,1)S(1)} %bitcast.103), kind=kOutput, calls=%fused_computation.48 | convolution fusion | flops 536870912 | bytes 10551296 | tf_op jit(solution)/shard_map/dot_general | solution.py:217
  341.0 15.1 %all-gather.2 = f32[8,66,256]{2,1,0:T(8,128)S(1)} all-gather(f32[1,66,256]{2,1,0:T(8,128)S(1)} %maximum_bitcast_fusion), channel_id=3, replica_groups=mesh['section'=4,'dp'=8] {'dp'}, dimensions={0}, use_global_device_ids=true | all-gather | bytes 608256 | tf_op jit(solution)/shard_map/all_gather | solution.py:227
  (57 shorter events, 9.1 us)
Async XLA Ops:
  7.2 94.4 %all-gather.6.cloned.1.call-start = ((), (), s32[]{:S(2)}) async-start(), calls=%async_computation.2 | async-start | bytes 9437184 | tf_op jit(solution)/shard_map/all_gather | solution.py:153
  14.7 2.0 copy-start.11
  14.7 2.2 copy-start.9
  14.7 2.2 copy-start.10
  15.4 86.1 %copy-start.1 = (bf16[2,1,4,16,4096]{4,3,2,1,0:T(8,128)(2,1)S(1)}, bf16[2,1,4,16,4096]{4,3,2,1,0:T(8,128)(2,1)}, u32[]{:S(2)}) copy-start(bf16[2,1,4,16,4096]{4,3,2,1,0:T(8,128)(2,1)} %param.9) | copy-start | bytes 3145732
  15.4 86.1 %copy-start.2 = (bf16[4,16,4096]{2,1,0:T(8,128)(2,1)S(1)}, bf16[4,16,4096]{2,1,0:T(8,128)(2,1)}, u32[]{:S(2)}) copy-start(bf16[4,16,4096]{2,1,0:T(8,128)(2,1)} %grad.1) | copy-start | bytes 1572868
  16.6 196.8 %reduce-scatter.5.cloned.1.call-start = ((), (), s32[]{:S(2)}) async-start(), calls=%async_computation.4 | async-start | bytes 4718592 | tf_op jit(solution)/shard_map/reduce_scatter | solution.py:208
  101.5 3.4 copy-start
  162.8 1.5 copy-start.3
  166.7 1.2 copy-start.4
  166.7 98.0 %reduce-scatter.3.cloned.1.call-start = ((), (), s32[]{:S(2)}) async-start(), calls=%async_computation.3 | async-start | bytes 4718592 | tf_op jit(solution)/shard_map/reduce_scatter | solution.py:208
  171.7 95.3 %copy-start.7 = (f32[2,1,8,256]{3,2,1,0:T(8,128)S(1)}, f32[2,1,8,256]{3,2,1,0:T(8,128)}, u32[]{:S(2)}) copy-start(f32[2,1,8,256]{3,2,1,0:T(8,128)} %param.15) | copy-start | bytes 49156
  171.7 146.5 %all-gather.8.cloned.1.call-start = ((), (), s32[]{:S(2)}) async-start(), calls=%async_computation.5 | async-start | bytes 5242880 | tf_op jit(solution)/shard_map/all_gather | solution.py:210
  324.2 3.5 copy-start.5
  327.7 2.2 copy-start.6
  329.3 2.3 copy-start.8
Sparse Core Ops, SparseCore 0:
  16.7 84.7 all-gather.5
  166.8 46.5 reduce-scatter.4
  216.3 48.3 reduce-scatter.2
  267.1 51.0 all-gather.7
where the time goes:
time: 365 us
  waiting for transfers between devices  220 us (60%)
  Pallas kernels  57.9 us (16%)
  blocking collectives  23.5 us (6%)
  matrix products  21.4 us (6%)
  local copies, waits for them, and re-layouts  19.8 us (5%)
  between operations  14 us (4%)
  other arithmetic  8.17 us (2%)
    reduce_scatter x2, waiting for transfers between devices, on_device(): lax.psum_scatter(pair, 'dp', scatter_dimension=0, tiled=True)  92.9 us
    all_gather x1, waiting for transfers between devices, on_device(): adapt = lax.all_gather(shard, 'dp', axis=0, tiled=True)  83.9 us
    pallas_call x1, Pallas kernels, on_device(): pl.pallas_call(functools.partial(relay, sections, blocks, micro, min(widt...  57.9 us
    all_gather x1, waiting for transfers between devices, on_device(): every = lax.all_gather(own, 'section', axis=0, tiled=True)  42.8 us
    all_gather x1, blocking collectives, on_device(): sums = jnp.sum(lax.all_gather(sums, 'dp', axis=0), axis=0)  15.1 us
    dot_general x2, matrix products, on_device(): lax.dot_general(cond_all, every[which], tn, preferred_element_type=jnp.fl...  9.34 us
    unnamed x27, local copies, waits for them, and re-layouts  8.6 us
    all_gather x1, blocking collectives, on_device(): slots = lax.all_gather(slot_embed[:, 0], 'section', axis=0)  8.39 us
  transfers between devices with their start and end apart: 4, of which 4 were waited for; matrix products, arithmetic and copies ran while one was open for 1% of the time, Pallas kernels for 0%

commit v1 on v0

v1 whole, which is shorter than its diff:
```python
import functools

import jax
import jax.numpy as jnp
from jax import lax
from jax.experimental import pallas as pl
from jax.experimental.pallas import tpu as pltpu
from jax.sharding import PartitionSpec as P

eps = 1e-05
MESH = pl.DeviceIdType.MESH
nt = (((1,), (1,)), ((), ()))
tn = (((0,), (0,)), ((), ()))
f32 = jnp.float32
bf = jnp.bfloat16


def backward(
    sizes,
    hid_in, grad_in, cols, cond_own, slots_own, task, gen_down, gen_up,
    hid_out, every, cond_all, slot_out, task_out,
    gens, hid, xn, inv_s, low_s, low_w, glow_s, landed, made, adapt, gpart, sibl, rland,
    slots_all, part, sums,
    gen_sem, in_sem, ag_send, ag_recv, sib_send, sib_recv, rsib_send, rsib_recv, rs_send, rs_recv,
    sec_send, sec_recv, rel_send, rel_recv, slot_send, slot_recv, sum_send, sum_recv,
):
    sections, ways, blocks, micro, tok, width, tasks, experts, per, cuts, piece = sizes
    me, d = lax.axis_index("section"), lax.axis_index("dp")
    chips = ways // 2
    z, c = d // 2, lax.rem(d, 2)
    pal = d + 1 - 2 * c
    last = chips - 1
    combos = tasks * experts
    rows = per * combos
    groups = ways // cuts
    ranks = groups * rows
    cond_width = gens.shape[1]
    chunk = min(piece, 1024)
    hop = width // 4
    tokens = micro * tok
    total = blocks * micro
    below, above = lax.rem(me + sections - 1, sections), lax.rem(me + 1, sections)
    scale = 1.0 / (micro * tok * ways)

    def remote(src, dst, send, recv, where):
        return pltpu.make_async_remote_copy(
            src_ref=src, dst_ref=dst, send_sem=send, recv_sem=recv,
            device_id=where, device_id_type=MESH,
        )

    def steps(low, high, body):
        def run(k, carry):
            body(k)
            return carry

        lax.fori_loop(low, high, run, 0)

    gen_copies = []
    for g, source in ((1, gen_up), (0, gen_down)):
        for n, at in enumerate(range(0, per * piece, chunk)):
            gen_copies.append(
                pltpu.make_async_copy(
                    source.at[:, pl.ds(at, chunk)], gens.at[g, :, pl.ds(at, chunk)], gen_sem.at[g, n]
                )
            )
            gen_copies[-1].start()
    hid_copy = pltpu.make_async_copy(hid_in, hid, in_sem.at[0])
    hid_copy.start()

    @pl.when(me == sections - 1)
    def _():
        pltpu.make_async_copy(grad_in, landed.at[pl.ds(0, micro)], in_sem.at[1]).start()

    barrier = pltpu.get_barrier_semaphore()

    def greet_dp(k):
        pl.semaphore_signal(
            barrier, inc=1, device_id={"dp": lax.rem(d + k, ways)}, device_id_type=MESH
        )

    def greet_section(k):
        pl.semaphore_signal(
            barrier, inc=1, device_id={"section": lax.rem(me + k, sections)}, device_id_type=MESH
        )

    steps(1, ways, greet_dp)
    steps(1, sections, greet_section)

    my_cut, my_group = lax.rem(d, cuts), d // cuts
    cond = cond_own[...]

    def generate(g):
        for n, at in enumerate(range(0, per * piece, chunk)):
            gen_copies[(1 - g) * (per * piece // chunk) + n].wait()
            out = jnp.dot(cond, gens[g, :, pl.ds(at, chunk)], preferred_element_type=f32).astype(bf)
            row, col = at // piece * combos, at % piece
            for b in range(blocks):
                adapt[b, g, my_cut, my_group, pl.ds(row, combos), pl.ds(col, chunk)] = out[
                    b * combos : (b + 1) * combos
                ]

    def shard(b, g, chip, core):
        dev = 2 * chip + core
        return adapt.at[b, g, lax.rem(dev, cuts), dev // cuts]

    def ag_hop(side, b, g, k, chip):
        ref = shard(b, g, chip, c)
        q = 2 * b + g
        to = d + 2 if side == 0 else d - 2
        return remote(
            ref, ref, ag_send.at[side, q, k - 1], ag_recv.at[side, q, k - 1], {"dp": to}
        )

    def ag_pal(b, g, chip, core):
        ref = shard(b, g, chip, core)
        q = 2 * b + g
        return remote(ref, ref, sib_send.at[q, chip], sib_recv.at[q, chip], {"dp": pal})

    def ag_start(b, g):
        @pl.when(z < last)
        def _():
            ag_hop(0, b, g, 1, z).start()

        @pl.when(z > 0)
        def _():
            ag_hop(1, b, g, 1, z).start()

        ag_pal(b, g, z, c).start()

    def ag_service(b, g, k):
        @pl.when(z >= k)
        def _():
            ag_hop(0, b, g, k, z - k).wait_recv()

            @pl.when((z < last) & (k < last))
            def _():
                ag_hop(0, b, g, k + 1, z - k).start()

            ag_pal(b, g, z - k, c).start()

        @pl.when(z + k <= last)
        def _():
            ag_hop(1, b, g, k, z + k).wait_recv()

            @pl.when((z > 0) & (k < last))
            def _():
                ag_hop(1, b, g, k + 1, z + k).start()

            ag_pal(b, g, z + k, c).start()

    def ag_finish(b, g):
        steps(0, chips, lambda chip: ag_pal(b, g, chip, 1 - c).wait_recv())

    def ag_drain(b, g):
        def one(k):
            @pl.when((z < last) & (z - k + 1 >= 0))
            def _():
                ag_hop(0, b, g, k, z - k + 1).wait_send()

            @pl.when((z > 0) & (z + k - 1 <= last))
            def _():
                ag_hop(1, b, g, k, z + k - 1).wait_send()

        steps(1, chips, one)
        steps(0, chips, lambda chip: ag_pal(b, g, chip, c).wait_send())

    def spans(size):
        for at in range(0, width, size):
            yield at, at // piece, at % piece

    def panel(b, g, at, size):
        return adapt[b, g, at // piece, :, :, pl.ds(at % piece, size)].reshape(ranks, size)

    def norm(b):
        square = jnp.zeros((tokens, 1), f32)
        for at, _, _ in spans(chunk):
            x = hid[b, :, pl.ds(at, chunk)].astype(f32)
            square += jnp.sum(x * x, axis=-1, keepdims=True)
        inv = lax.rsqrt(square * (1.0 / width) + eps)
        inv_s[b] = inv
        for at, _, _ in spans(chunk):
            xn[b, :, pl.ds(at, chunk)] = (hid[b, :, pl.ds(at, chunk)].astype(f32) * inv).astype(bf)

    def project(b):
        low = jnp.zeros((tokens, ranks), f32)
        for at, _, _ in spans(chunk):
            low += lax.dot_general(
                xn[b, :, pl.ds(at, chunk)], panel(b, 0, at, chunk), nt, preferred_element_type=f32
            )
        low_s[b] = low
        low_w[b] = (cols[b] * low).astype(bf)

    def relay_hop(item, slot, n):
        at = pl.ds(n * hop, hop)
        return remote(
            made.at[item, :, at], landed.at[slot, :, at],
            rel_send.at[item, n], rel_recv.at[slot, n], {"section": below},
        )

    def relay(b):
        first_item = (blocks - 1 - b) * micro

        def one(m):
            item = first_item + m
            mine = pl.ds(pl.multiple_of(m * tok, tok), tok)
            back = jnp.zeros((tok, ranks), f32)
            for n in range(4):
                if b == blocks - 1:
                    @pl.when(me < sections - 1)
                    def _():
                        relay_hop(item, item, n).wait_recv()
                else:
                    relay_hop(item, item, n).wait_recv()
                for at in range(n * hop, (n + 1) * hop, min(hop, chunk)):
                    back += lax.dot_general(
                        landed[item, :, pl.ds(at, min(hop, chunk))], panel(b, 1, at, min(hop, chunk)),
                        nt, preferred_element_type=f32,
                    )
            glow = (cols[b, mine] * back).astype(bf)
            glow_s[b, mine] = glow
            dots = jnp.sum(glow.astype(f32) * low_s[b, mine], axis=-1, keepdims=True) * (1.0 / width)
            inv = inv_s[b, mine]
            scaled = dots * inv
            for n in range(4):
                for at in range(n * hop, (n + 1) * hop, min(hop, chunk)):
                    size = min(hop, chunk)
                    up = jnp.dot(glow, panel(b, 0, at, size), preferred_element_type=f32)
                    xf = hid[b, mine, pl.ds(at, size)].astype(f32) * inv
                    dx = landed[item, :, pl.ds(at, size)].astype(f32) + (inv * up - xf * scaled)
                    dx = dx.astype(bf)
                    made[item, :, pl.ds(at, size)] = dx
                    if b == 0:
                        hid_out[m, :, pl.ds(at, size)] = dx

                @pl.when(me > 0)
                def _():
                    relay_hop(item, item, n).start()

                if b > 0:
                    @pl.when(me == 0)
                    def _():
                        relay_hop(item, item + micro, n).start()

        steps(0, micro, one)

    def relay_drain(item):
        for n in range(4):
            @pl.when((me > 0) | (item < total - micro))
            def _():
                relay_hop(item, item, n).wait_send()

    def grads(b, g):
        base = (blocks - 1 - b) * micro
        left = (glow_s if g == 0 else low_w)[b]
        for at, cut, col in spans(chunk):
            if g == 0:
                right = xn[b, :, pl.ds(at, chunk)]
            else:
                right = landed[pl.ds(base, micro), :, pl.ds(at, chunk)].reshape(tokens, chunk)
            out = lax.dot_general(left, right, tn, preferred_element_type=f32) * scale
            gpart[b, g, cut, :, :, pl.ds(col, chunk)] = out.astype(bf).reshape(groups, rows, chunk)

    def bucket(b, g, chip, core):
        dev = 2 * chip + core
        return gpart.at[b, g, lax.rem(dev, cuts), dev // cuts]

    def rs_pal(b, g, chip, core):
        q = 2 * b + g
        return remote(
            bucket(b, g, chip, core), sibl.at[q, chip],
            rsib_send.at[q, chip], rsib_recv.at[q, chip], {"dp": pal},
        )

    def rs_hop(side, b, g, k, dest):
        q = 2 * b + g
        to = d + 2 if side == 0 else d - 2
        return remote(
            bucket(b, g, dest, c), rland.at[side, q, k - 1],
            rs_send.at[side, q, k - 1], rs_recv.at[side, q, k - 1], {"dp": to},
        )

    def add_into(target, *others):
        for at in range(0, piece, chunk):
            value = target[:, pl.ds(at, chunk)].astype(f32)
            for other in others:
                value = value + other[:, pl.ds(at, chunk)].astype(f32)
            target[:, pl.ds(at, chunk)] = value.astype(bf)

    def rs_exchange(b, g):
        steps(0, chips, lambda chip: rs_pal(b, g, chip, 1 - c).start())

    def rs_start(b, g):
        def one(chip):
            rs_pal(b, g, chip, c).wait_recv()
            add_into(bucket(b, g, chip, c), sibl.at[2 * b + g, chip])

        steps(0, chips, one)

        @pl.when(z == 0)
        def _():
            steps(1, chips, lambda k: rs_hop(0, b, g, k, chips - k).start())

        @pl.when(z == last)
        def _():
            steps(1, chips, lambda k: rs_hop(1, b, g, k, k - 1).start())

    def rs_service(b, g, k):
        q = 2 * b + g

        @pl.when((z >= 1) & (k >= z) & (k < last))
        def _():
            dest = chips - k + z - 1
            rs_hop(0, b, g, k, dest).wait_recv()
            add_into(bucket(b, g, dest, c), rland.at[0, q, k - 1])
            rs_hop(0, b, g, k + 1, dest).start()

        @pl.when((z < last) & (k >= last - z) & (k < last))
        def _():
            dest = z + k - last
            rs_hop(1, b, g, k, dest).wait_recv()
            add_into(bucket(b, g, dest, c), rland.at[1, q, k - 1])
            rs_hop(1, b, g, k + 1, dest).start()

    def rs_finish(b, g):
        q = 2 * b + g

        @pl.when(z >= 1)
        def _():
            rs_hop(0, b, g, last, z).wait_recv()

        @pl.when(z < last)
        def _():
            rs_hop(1, b, g, last, z).wait_recv()

        own = bucket(b, g, z, c)

        def put(*others):
            for at in range(0, piece, chunk):
                value = own[:, pl.ds(at, chunk)].astype(f32)
                for other in others:
                    value = value + other[:, pl.ds(at, chunk)].astype(f32)
                every[me, b, g, :, pl.ds(at, chunk)] = value.astype(bf)

        @pl.when(z == 0)
        def _():
            put(rland.at[1, q, last - 1])

        @pl.when(z == last)
        def _():
            put(rland.at[0, q, last - 1])

        @pl.when((z > 0) & (z < last))
        def _():
            put(rland.at[0, q, last - 1], rland.at[1, q, last - 1])

    def rs_drain(b, g):
        steps(0, chips, lambda chip: rs_pal(b, g, chip, 1 - c).wait_send())

        def one(k):
            @pl.when(k >= z + 1)
            def _():
                rs_hop(0, b, g, k, chips - k + z).wait_send()

            @pl.when(k >= chips - z)
            def _():
                rs_hop(1, b, g, k, k - chips + z).wait_send()

        steps(1, chips, one)

    def sec_hop(b, g, k, owner):
        q = 2 * b + g
        ref = every.at[owner, b, g]
        return remote(
            ref, ref, sec_send.at[q, k - 1], sec_recv.at[q, k - 1],
            {"section": lax.rem(me + k, sections)},
        )

    def sec_start(b, g):
        for k in range(1, sections):
            sec_hop(b, g, k, me).start()

    def sec_finish(b, g):
        for k in range(1, sections):
            sec_hop(b, g, k, lax.rem(me + sections - k, sections)).wait_recv()

    def sec_drain(b, g):
        for k in range(1, sections):
            sec_hop(b, g, k, me).wait_send()

    def contract(b, g):
        out = jnp.zeros((sections * combos, cond_width), f32)
        for at in range(0, per * piece, chunk):
            row, col = at // piece * combos, at % piece
            left = every[:, b, g, pl.ds(row, combos), pl.ds(col, chunk)]
            out += lax.dot_general(
                left.reshape(sections * combos, chunk), gens[g, :, pl.ds(at, chunk)], nt,
                preferred_element_type=f32,
            )
        part[:, b] += out.reshape(sections, combos, cond_width)

    def slot_hop(k, owner):
        ref = slots_all.at[owner]
        return remote(
            slots_own, ref, slot_send.at[k - 1], slot_recv.at[k - 1],
            {"section": lax.rem(me + k, sections)},
        )

    def sum_hop(k):
        return remote(
            sums.at[d], sums.at[d], sum_send.at[k - 1], sum_recv.at[d],
            {"dp": lax.rem(d + k, ways)},
        )

    top, kinds = blocks - 1, (1, 0)
    generate(1)
    pl.semaphore_wait(barrier, ways - 1 + sections - 1)
    ag_start(top, 1)
    generate(0)
    ag_start(top, 0)
    for k in range(1, sections):
        slot_hop(k, me).start()
    hid_copy.wait()
    for b in reversed(range(blocks)):
        norm(b)
    part[...] = jnp.zeros_like(part)

    def both(fn, *args):
        for g in kinds:
            fn(*args[:1], g, *args[1:])

    steps(1, chips, lambda k: both(ag_service, top, k))
    for b in reversed(range(top)):
        both(ag_start, b)
    both(ag_finish, top)
    project(top)

    @pl.when(me == sections - 1)
    def _():
        pltpu.make_async_copy(grad_in, landed.at[pl.ds(0, micro)], in_sem.at[1]).wait()

    for b in reversed(range(blocks)):
        if b > 0:
            early = me < sections // 2

            @pl.when(early)
            def _():
                both(ag_service, b - 1, 1)

        relay(b)
        if b > 0:
            @pl.when(jnp.logical_not(early))
            def _():
                both(ag_service, b - 1, 1)

        for g in (0, 1):
            grads(b, g)
        if b > 0:
            steps(2, last, lambda k: both(ag_service, b - 1, k))
            for g in (0, 1):
                rs_exchange(b, g)
            for g in (0, 1):
                rs_start(b, g)
            if last > 1:
                both(ag_service, b - 1, last)
            both(ag_finish, b - 1)
            project(b - 1)
        else:
            for g in (0, 1):
                rs_exchange(b, g)
        if b == top:
            continue
        for g in (0, 1):
            steps(1, last, lambda k: rs_service(b + 1, g, k))
        for g in (0, 1):
            if b == 0:
                rs_start(b, g)
        for g in (0, 1):
            rs_finish(b + 1, g)
            sec_start(b + 1, g)
    for k in range(1, sections):
        slot_hop(k, lax.rem(me + sections - k, sections)).wait_recv()
    slots_all[me] = slots_own[...]
    pre = task[...][None, None, :, None, :] + slots_all[...][:, :, None, :, :]
    sig = 1.0 / (1.0 + jnp.exp(-pre))
    cond_all[...] = (pre * sig).reshape(sections * blocks * combos, cond_width).astype(bf)
    slope = sig * (1.0 + pre * (1.0 - sig))
    for b in range(1, blocks):
        for g in (0, 1):
            sec_finish(b, g)
            contract(b, g)
    for g in (0, 1):
        steps(1, last, lambda k: rs_service(0, g, k))
        rs_finish(0, g)
        sec_start(0, g)
    for g in (0, 1):
        sec_finish(0, g)
        contract(0, g)

    d_pre = part[...].reshape(sections, blocks, tasks, experts, cond_width) * slope
    part[...] = d_pre.reshape(sections, blocks, combos, cond_width)
    own = part[me].reshape(blocks, tasks, experts, cond_width)
    sums[d] = jnp.zeros_like(sums[d])
    sums[d, pl.ds(0, blocks * experts)] = jnp.sum(own, axis=1).reshape(blocks * experts, cond_width)
    sums[d, pl.ds(blocks * experts, tasks)] = jnp.sum(d_pre, axis=(0, 1, 3))
    steps(1, ways, lambda k: sum_hop(k).start())

    for b in range(blocks):
        for g in (0, 1):
            ag_drain(b, g)
            rs_drain(b, g)
            sec_drain(b, g)
    steps(0, total, relay_drain)
    for k in range(1, sections):
        slot_hop(k, me).wait_send()

    def sum_wait(k):
        other = lax.rem(d + k, ways)
        remote(
            sums.at[other], sums.at[other], sum_send.at[k - 1], sum_recv.at[other],
            {"dp": other},
        ).wait_recv()

    steps(1, ways, sum_wait)
    steps(1, ways, lambda k: sum_hop(k).wait_send())
    whole = jnp.sum(sums[...], axis=0)
    slot_out[...] = whole[: blocks * experts]
    task_out[...] = whole[blocks * experts : blocks * experts + tasks]


def generators(cond, every, down, up):
    rows = cond.shape[0]
    for g, out in ((0, down), (1, up)):
        right = every[:, :, g].reshape(rows, every.shape[-1])
        out[...] = lax.dot_general(cond[...], right, tn, preferred_element_type=f32)


def on_device(
    hidden_in, out_grad, gate_probs, expert_ids, task_ids, task_embed, slot_embed, gen_down, gen_up
):
    sections, ways = lax.axis_size("section"), lax.axis_size("dp")
    blocks, _, micro, tok, width = hidden_in.shape
    tasks, cond_width = task_embed.shape
    experts = slot_embed.shape[2]
    combos = tasks * experts
    span = gen_down.shape[1]
    per = max(1, span // width)
    cuts = max(1, width // span)
    piece = span // per
    rows = per * combos
    groups = ways // cuts
    ranks = groups * rows
    total, tokens, chips = blocks * micro, micro * tok, ways // 2
    quads = 2 * blocks
    chunk = min(piece, 1024)

    slots_own = slot_embed[:, 0]
    pre_own = task_embed[None, :, None, :] + slots_own[:, None, :, :]
    cond_own = jax.nn.silu(pre_own).reshape(-1, cond_width).astype(bf)
    hot = (expert_ids[:, 0][..., None] == jnp.arange(experts, dtype=jnp.int32)).astype(f32)
    per_expert = jnp.sum(gate_probs[:, 0][..., None] * hot, axis=3)
    task_hot = (task_ids == jnp.arange(tasks, dtype=jnp.int32)).astype(f32)
    table = task_hot[None, :, None, :, None] * per_expert[:, :, :, None, :]
    cols = jnp.tile(table.reshape(blocks, tokens, combos), (1, 1, ranks // combos))

    vmem = pl.BlockSpec(memory_space=pltpu.VMEM)
    anywhere = pl.BlockSpec(memory_space=pl.ANY)
    sem = pltpu.SemaphoreType.DMA
    sizes = (sections, ways, blocks, micro, tok, width, tasks, experts, per, cuts, piece)
    hid_out, every, cond_all, d_slot, d_task = pl.pallas_call(
        functools.partial(backward, sizes),
        out_shape=(
            jax.ShapeDtypeStruct((micro, tok, width), bf),
            jax.ShapeDtypeStruct((sections, blocks, 2, rows, piece), bf),
            jax.ShapeDtypeStruct((sections * blocks * combos, cond_width), bf),
            jax.ShapeDtypeStruct((blocks * experts, cond_width), f32),
            jax.ShapeDtypeStruct((tasks, cond_width), f32),
        ),
        in_specs=[anywhere, anywhere, vmem, vmem, vmem, vmem, anywhere, anywhere],
        out_specs=(vmem,) * 5,
        scratch_shapes=[
            pltpu.VMEM((2, cond_width, span), bf),
            pltpu.VMEM((blocks, tokens, width), bf),
            pltpu.VMEM((blocks, tokens, width), bf),
            pltpu.VMEM((blocks, tokens, 1), f32),
            pltpu.VMEM((blocks, tokens, ranks), f32),
            pltpu.VMEM((blocks, tokens, ranks), bf),
            pltpu.VMEM((blocks, tokens, ranks), bf),
            pltpu.VMEM((total, tok, width), bf),
            pltpu.VMEM((total, tok, width), bf),
            pltpu.VMEM((blocks, 2, cuts, groups, rows, piece), bf),
            pltpu.VMEM((blocks, 2, cuts, groups, rows, piece), bf),
            pltpu.VMEM((quads, chips, rows, piece), bf),
            pltpu.VMEM((2, quads, chips - 1, rows, piece), bf),
            pltpu.VMEM((sections, blocks, experts, cond_width), f32),
            pltpu.VMEM((sections, blocks, combos, cond_width), f32),
            pltpu.VMEM((ways, blocks * experts + 8, cond_width), f32),
            sem((2, span // chunk)),
            sem((2,)),
            sem((2, quads, chips - 1)),
            sem((2, quads, chips - 1)),
            sem((quads, chips)),
            sem((quads, chips)),
            sem((quads, chips)),
            sem((quads, chips)),
            sem((2, quads, chips - 1)),
            sem((2, quads, chips - 1)),
            sem((quads, sections - 1)),
            sem((quads, sections - 1)),
            sem((total, 4)),
            sem((total, 4)),
            sem((sections - 1,)),
            sem((sections - 1,)),
            sem((ways - 1,)),
            sem((ways,)),
        ],
        compiler_params=pltpu.CompilerParams(
            collective_id=1, has_side_effects=True, vmem_limit_bytes=58 << 20
        ),
        name="backward",
    )(
        hidden_in.reshape(blocks, tokens, width), out_grad, cols, cond_own, slots_own, task_embed,
        gen_down, gen_up,
    )

    out_chunk = min(piece, 1024)
    d_down, d_up = pl.pallas_call(
        generators,
        grid=(per, piece // out_chunk),
        out_shape=(jax.ShapeDtypeStruct((cond_width, span), f32),) * 2,
        in_specs=[
            pl.BlockSpec((sections * blocks * combos, cond_width), lambda p, i: (0, 0)),
            pl.BlockSpec((sections, blocks, 2, combos, out_chunk), lambda p, i: (0, 0, 0, p, i)),
        ],
        out_specs=(
            pl.BlockSpec((cond_width, out_chunk), lambda p, i: (0, p * (piece // out_chunk) + i)),
        ) * 2,
        compiler_params=pltpu.CompilerParams(vmem_limit_bytes=24 << 20),
        name="generators",
    )(cond_all, every)
    return (
        hid_out[None], d_down, d_up, d_task,
        d_slot.reshape(blocks, 1, experts, cond_width),
    )


def solution(mesh):
    placed = (
        P(None, "section", None, "dp", None),
        P(None, "dp", None),
        P(None, "section", None, "dp", None),
        P(None, "section", None, "dp", None),
        P(None, "dp"),
        P(),
        P(None, "section", None, None),
        P(None, "dp"),
        P(None, "dp"),
    )
    return jax.shard_map(
        on_device,
        mesh=mesh,
        in_specs=placed,
        out_specs=(
            P("section", None, "dp", None),
            P(None, "dp"),
            P(None, "dp"),
            P(),
            P(None, "section", None, None),
        ),
        check_vma=False,
    )
```

time: 365 us -> 200 us (0.55)
  waiting for transfers between devices: 220 us -> 0 us
  Pallas kernels: 57.9 us -> 190 us
  blocking collectives: 23.5 us -> 0 us
  matrix products: 21.4 us -> 0 us
  local copies, waits for them, and re-layouts: 19.8 us -> 6.07 us
  between operations: 14 us -> 0.69 us
  other arithmetic: 8.17 us -> 2.76 us
    pallas_call x1 -> x2, Pallas kernels: 57.9 us -> 190 us  [the longest x1 183 us: on_device(): pl.pallas_call(functools.partial(backward, sizes), out_shape=(jax.ShapeDt...]
    all_gather x2 -> x0, waiting for transfers between devices: 127 us -> none  [the longest x1 83.9 us: on_device(): adapt = lax.all_gather(shard, 'dp', axis=0, tiled=True)]
    reduce_scatter x2 -> x0, waiting for transfers between devices: 92.9 us -> none  [on_device(): lax.psum_scatter(pair, 'dp', scatter_dimension=0, tiled=True)]
    all_gather x2 -> x0, blocking collectives: 23.5 us -> none  [the longest x1 15.1 us: on_device(): sums = jnp.sum(lax.all_gather(sums, 'dp', axis=0), axis=0)]
    dot_general x10 -> x0, matrix products: 21.4 us -> none  [the longest x2 9.34 us: on_device(): lax.dot_general(cond_all, every[which], tn, preferred_element_type=jnp.fl...]
    slice x4 -> x0, local copies, waits for them, and re-layouts: 7.45 us -> none  [the longest x3 6.87 us: on_device(): every[which]]
    concatenate x3 -> x0, other arithmetic: 7.02 us -> none  [the longest x2 4.75 us: on_device(): jnp.concatenate([grads(glow[at], xn[at]), grads(low[at], cot[at])], axis=1)]
    unnamed x27 -> x13, local copies, waits for them, and re-layouts: 8.6 us -> 5.01 us
  transfers between devices with their start and end apart: 4 -> 0, of which waited for: 4 -> 0; matrix products, arithmetic and copies ran while one was open for 1% -> 0% of each run, Pallas kernels for 0% -> 0%
where the time goes in v1:
time: 200 us
  Pallas kernels  190 us (95%)
  local copies, waits for them, and re-layouts  6.07 us (3%)
  other arithmetic  2.76 us (1%)
    pallas_call x1, Pallas kernels, on_device(): pl.pallas_call(functools.partial(backward, sizes), out_shape=(jax.ShapeDt...  183 us
    pallas_call x1, Pallas kernels, on_device(): pl.pallas_call(generators, grid=(per, piece // out_chunk), out_shape=(jax...  7.29 us
    unnamed x13, local copies, waits for them, and re-layouts  5.01 us

profile of v1, /device:TPU:0, one launch (start us, length us, event | category | flops | bytes accessed | tf_op | source)
XLA Modules:
  0.0 199.6 jit_solution(14385332190405079854)
XLA Ops:
  0.6 0.7 compare_convert_fusion
  1.3 0.1 mul.38
  1.4 0.1 mul.39
  1.4 0.7 select_reduce_fusion
  2.2 0.1 mul.45
  2.3 0.7 broadcast_add_fusion
  3.1 0.6 fusion.3.cond_own
  3.7 0.8 copy.22.cols
  4.5 182.8 %backward.1 = (bf16[4,16,4096]{2,1,0:T(8,128)(2,1)}, bf16[4,2,2,32,4096]{4,3,2,1,0:T(8,128)(2,1)}, bf16[128,256]{1,0:T(8,128)(2,1)}, f32[16,256]{1,0:T(8,128)}, f32[2,256]{1,0:T(2,128)}) custom-call(bf16[2,64,4096]{2,1,0:T(8,128)(2,1)} %bitcast.28, bf16[4,16,4096]{2,1,0:T(8,128)(2,1)} %grad_in.1, f32[2,64,256]{2,1,0:T(8,128)} %copy.22.cols, ...), custom_call_target="tpu_custom_call" | custom-call | tf_op jit(solution)/shard_map/backward/pallas_call | solution.py:569
  187.3 0.0 copy-start.4
  187.3 0.0 copy-start
  187.3 2.2 %copy-done = bf16[4,2,2,32,4096]{4,3,2,1,0:T(8,128)(2,1)S(1)} copy-done((bf16[4,2,2,32,4096]{4,3,2,1,0:T(8,128)(2,1)S(1)}, bf16[4,2,2,32,4096]{4,3,2,1,0:T(8,128)(2,1)}, u32[]{:S(2)}) %copy-start) | copy-done | bytes 4194328
  189.5 0.0 copy-start.1
  189.5 0.8 copy-done.1
  190.4 0.0 copy-start.2
  190.4 0.0 copy-start.3
  190.4 7.3 %generators.1 = (f32[256,8192]{1,0:T(8,128)}, f32[256,8192]{1,0:T(8,128)}) custom-call(bf16[128,256]{1,0:T(8,128)(2,1)S(1)} %copy-done.1, bf16[4,2,2,32,4096]{4,3,2,1,0:T(8,128)(2,1)S(1)} %copy-done), custom_call_target="tpu_custom_call" | custom-call | tf_op jit(solution)/shard_map/generators/pallas_call | solution.py:626
  197.7 0.0 copy-done.2
  197.7 0.8 copy.27
  198.5 0.0 copy-done.4
  198.5 0.6 copy.28
  199.0 0.0 copy-done.3
  199.0 0.6 copy.29
  (4 shorter events, 0.0 us)
Async XLA Ops:
  187.3 11.1 %copy-start.4 = (f32[2,256]{1,0:T(2,128)S(1)}, f32[2,256]{1,0:T(2,128)}, u32[]{:S(2)}) copy-start(f32[2,256]{1,0:T(2,128)} %get-tuple-element.42) | copy-start | bytes 6148
  187.3 2.2 %copy-start = (bf16[4,2,2,32,4096]{4,3,2,1,0:T(8,128)(2,1)S(1)}, bf16[4,2,2,32,4096]{4,3,2,1,0:T(8,128)(2,1)}, u32[]{:S(2)}) copy-start(bf16[4,2,2,32,4096]{4,3,2,1,0:T(8,128)(2,1)} %get-tuple-element.14.every) | copy-start | bytes 12582916
  189.5 0.8 copy-start.1
  190.4 7.3 %copy-start.2 = (bf16[4,16,4096]{2,1,0:T(8,128)(2,1)S(1)}, bf16[4,16,4096]{2,1,0:T(8,128)(2,1)}, u32[]{:S(2)}) copy-start(bf16[4,16,4096]{2,1,0:T(8,128)(2,1)} %get-tuple-element.12) | copy-start | bytes 1572868
  190.4 8.7 %copy-start.3 = (f32[16,256]{1,0:T(8,128)S(1)}, f32[16,256]{1,0:T(8,128)}, u32[]{:S(2)}) copy-start(f32[16,256]{1,0:T(8,128)} %get-tuple-element.18) | copy-start | bytes 49156

commit v2 on v1

v2 whole, which is shorter than its diff:
```python
import functools

import jax
import jax.numpy as jnp
from jax import lax
from jax.experimental import pallas as pl
from jax.experimental.pallas import tpu as pltpu
from jax.sharding import PartitionSpec as P

eps = 1e-05
MESH = pl.DeviceIdType.MESH
nt = (((1,), (1,)), ((), ()))
tn = (((0,), (0,)), ((), ()))
f32 = jnp.float32
bf = jnp.bfloat16


def backward(
    sizes,
    hid_in, grad_in, gates, picks, task_ids, slots_own, task, gen_down, gen_up,
    hid_out, every, cond_all, slot_out, task_out,
    gens, hid, xn, inv_s, low_s, low_w, glow_s, landed, made, adapt, gpart, sibl, rland,
    cols, reduced, slots_all, part, sums,
    gen_sem, in_sem, out_sem, put_sem, ag_send, ag_recv, sib_send, sib_recv, rsib_send, rsib_recv, rs_send, rs_recv,
    sec_send, sec_recv, rel_send, rel_recv, slot_send, slot_recv, sum_send, sum_recv,
    task_send, task_recv,
):
    sections, ways, blocks, micro, tok, width, tasks, experts, per, cuts, piece = sizes
    me, d = lax.axis_index("section"), lax.axis_index("dp")
    chips = ways // 2
    z, c = d // 2, lax.rem(d, 2)
    pal = d + 1 - 2 * c
    last = chips - 1
    combos = tasks * experts
    rows = per * combos
    groups = ways // cuts
    ranks = groups * rows
    cond_width = gens.shape[1]
    chunk = min(piece, 1024)
    hop = width // 4
    parts = rland.shape[1] // (2 * blocks)
    sub = piece // parts
    strip = min(sub, 1024)
    tokens = micro * tok
    total = blocks * micro
    below, above = lax.rem(me + sections - 1, sections), lax.rem(me + 1, sections)
    scale = 1.0 / (micro * tok * ways)

    def remote(src, dst, send, recv, where):
        return pltpu.make_async_remote_copy(
            src_ref=src, dst_ref=dst, send_sem=send, recv_sem=recv,
            device_id=where, device_id_type=MESH,
        )

    def steps(low, high, body):
        def run(k, carry):
            body(k)
            return carry

        lax.fori_loop(low, high, run, 0)

    gen_copies = []
    for g, source in ((1, gen_up), (0, gen_down)):
        for n, at in enumerate(range(0, per * piece, chunk)):
            gen_copies.append(
                pltpu.make_async_copy(
                    source.at[:, pl.ds(at, chunk)], gens.at[g, :, pl.ds(at, chunk)], gen_sem.at[g, n]
                )
            )
            gen_copies[-1].start()
    hid_copy = pltpu.make_async_copy(hid_in, hid, in_sem.at[0])
    hid_copy.start()

    @pl.when(me == sections - 1)
    def _():
        pltpu.make_async_copy(grad_in, landed.at[pl.ds(0, micro)], in_sem.at[1]).start()

    barrier = pltpu.get_barrier_semaphore()

    def greet_dp(k):
        pl.semaphore_signal(
            barrier, inc=1, device_id={"dp": lax.rem(d + k, ways)}, device_id_type=MESH
        )

    def greet_section(k):
        pl.semaphore_signal(
            barrier, inc=1, device_id={"section": lax.rem(me + k, sections)}, device_id_type=MESH
        )

    steps(1, ways, greet_dp)
    steps(1, sections, greet_section)

    my_cut, my_group = lax.rem(d, cuts), d // cuts
    pre = task[...][None, :, None, :] + slots_own[...][:, None, :, :]
    sig = 1.0 / (1.0 + jnp.exp(-pre))
    cond = (pre * sig).reshape(blocks * combos, cond_width).astype(bf)

    def weigh():
        eye = lax.broadcasted_iota(jnp.int32, (tok, tok), 0) == lax.broadcasted_iota(
            jnp.int32, (tok, tok), 1
        )
        lane = lax.broadcasted_iota(jnp.int32, (tok, ranks), 1)
        expert = lax.rem(lane, experts).astype(f32)
        task_of = lax.rem(lane, combos) // experts

        def column(row):
            return jnp.sum(jnp.where(eye, row, 0.0), axis=1, keepdims=True)

        for m in range(micro):
            right_task = jnp.where(task_of == task_ids[m, 0], 1.0, 0.0)
            for b in range(blocks):
                total_weight = jnp.zeros((tok, ranks), f32)
                for k in range(gates.shape[2]):
                    pick = column(picks[b, m, k : k + 1].astype(f32))
                    gate = column(gates[b, m, k : k + 1])
                    total_weight += jnp.where(pick == expert, gate, 0.0)
                cols[b, m * tok : (m + 1) * tok] = right_task * total_weight

    def generate(g):
        for n, at in enumerate(range(0, per * piece, chunk)):
            gen_copies[(1 - g) * (per * piece // chunk) + n].wait()
            out = jnp.dot(cond, gens[g, :, pl.ds(at, chunk)], preferred_element_type=f32).astype(bf)
            row, col = at // piece * combos, at % piece
            for b in range(blocks):
                adapt[b, g, my_cut, my_group, pl.ds(row, combos), pl.ds(col, chunk)] = out[
                    b * combos : (b + 1) * combos
                ]

    def shard(b, g, chip, core):
        dev = 2 * chip + core
        return adapt.at[b, g, lax.rem(dev, cuts), dev // cuts]

    def ag_hop(side, b, g, k, chip):
        ref = shard(b, g, chip, c)
        q = 2 * b + g
        to = d + 2 if side == 0 else d - 2
        return remote(
            ref, ref, ag_send.at[side, q, k - 1], ag_recv.at[side, q, k - 1], {"dp": to}
        )

    def ag_pal(b, g, chip, core):
        ref = shard(b, g, chip, core)
        q = 2 * b + g
        return remote(ref, ref, sib_send.at[q, chip], sib_recv.at[q, chip], {"dp": pal})

    def ag_start(b, g):
        @pl.when(z < last)
        def _():
            ag_hop(0, b, g, 1, z).start()

        @pl.when(z > 0)
        def _():
            ag_hop(1, b, g, 1, z).start()

        ag_pal(b, g, z, c).start()

    def ag_service(b, g, k):
        @pl.when(z >= k)
        def _():
            ag_hop(0, b, g, k, z - k).wait_recv()

            @pl.when((z < last) & (k < last))
            def _():
                ag_hop(0, b, g, k + 1, z - k).start()

            ag_pal(b, g, z - k, c).start()

        @pl.when(z + k <= last)
        def _():
            ag_hop(1, b, g, k, z + k).wait_recv()

            @pl.when((z > 0) & (k < last))
            def _():
                ag_hop(1, b, g, k + 1, z + k).start()

            ag_pal(b, g, z + k, c).start()

    def ag_finish(b, g):
        steps(0, chips, lambda chip: ag_pal(b, g, chip, 1 - c).wait_recv())

    def ag_drain(b, g):
        def one(k):
            @pl.when((z < last) & (z - k + 1 >= 0))
            def _():
                ag_hop(0, b, g, k, z - k + 1).wait_send()

            @pl.when((z > 0) & (z + k - 1 <= last))
            def _():
                ag_hop(1, b, g, k, z + k - 1).wait_send()

        steps(1, chips, one)
        steps(0, chips, lambda chip: ag_pal(b, g, chip, c).wait_send())

    def spans(size):
        for at in range(0, width, size):
            yield at, at // piece, at % piece

    def panel(b, g, at, size):
        return adapt[b, g, at // piece, :, :, pl.ds(at % piece, size)].reshape(ranks, size)

    def norm(b):
        square = jnp.zeros((tokens, 1), f32)
        for at, _, _ in spans(chunk):
            x = hid[b, :, pl.ds(at, chunk)].astype(f32)
            square += jnp.sum(x * x, axis=-1, keepdims=True)
        inv = lax.rsqrt(square * (1.0 / width) + eps)
        inv_s[b] = inv
        for at, _, _ in spans(chunk):
            xn[b, :, pl.ds(at, chunk)] = (hid[b, :, pl.ds(at, chunk)].astype(f32) * inv).astype(bf)

    def project(b):
        low = jnp.zeros((tokens, ranks), f32)
        for at, _, _ in spans(chunk):
            low += lax.dot_general(
                xn[b, :, pl.ds(at, chunk)], panel(b, 0, at, chunk), nt, preferred_element_type=f32
            )
        low_s[b] = low
        low_w[b] = (cols[b] * low).astype(bf)

    def relay_hop(item, slot, n):
        at = pl.ds(n * hop, hop)
        return remote(
            made.at[item, :, at], landed.at[slot, :, at],
            rel_send.at[item, n], rel_recv.at[slot, n], {"section": below},
        )

    def hid_put(m):
        return pltpu.make_async_copy(
            made.at[total - micro + m], hid_out.at[m], out_sem.at[m]
        )

    def relay(b, between):
        first_item = (blocks - 1 - b) * micro

        def one(m):
            item = first_item + m
            between(m)
            mine = pl.ds(pl.multiple_of(m * tok, tok), tok)
            back = jnp.zeros((tok, ranks), f32)
            for n in range(4):
                if b == blocks - 1:
                    @pl.when(me < sections - 1)
                    def _():
                        relay_hop(item, item, n).wait_recv()
                else:
                    relay_hop(item, item, n).wait_recv()
                for at in range(n * hop, (n + 1) * hop, min(hop, chunk)):
                    back += lax.dot_general(
                        landed[item, :, pl.ds(at, min(hop, chunk))], panel(b, 1, at, min(hop, chunk)),
                        nt, preferred_element_type=f32,
                    )
            glow = (cols[b, mine] * back).astype(bf)
            glow_s[b, mine] = glow
            dots = jnp.sum(glow.astype(f32) * low_s[b, mine], axis=-1, keepdims=True) * (1.0 / width)
            inv = inv_s[b, mine]
            scaled = dots * inv
            for n in range(4):
                for at in range(n * hop, (n + 1) * hop, min(hop, chunk)):
                    size = min(hop, chunk)
                    up = jnp.dot(glow, panel(b, 0, at, size), preferred_element_type=f32)
                    xf = hid[b, mine, pl.ds(at, size)].astype(f32) * inv
                    dx = landed[item, :, pl.ds(at, size)].astype(f32) + (inv * up - xf * scaled)
                    dx = dx.astype(bf)
                    made[item, :, pl.ds(at, size)] = dx

                @pl.when(me > 0)
                def _():
                    relay_hop(item, item, n).start()

                if b > 0:
                    @pl.when(me == 0)
                    def _():
                        relay_hop(item, item + micro, n).start()

            if b == 0:
                hid_put(m).start()

        steps(0, micro, one)

    def relay_drain(item):
        for n in range(4):
            @pl.when((me > 0) | (item < total - micro))
            def _():
                relay_hop(item, item, n).wait_send()

    def grads(b, g):
        base = (blocks - 1 - b) * micro
        left = (glow_s if g == 0 else low_w)[b]
        for at, cut, col in spans(chunk):
            if g == 0:
                right = xn[b, :, pl.ds(at, chunk)]
            else:
                right = landed[pl.ds(base, micro), :, pl.ds(at, chunk)].reshape(tokens, chunk)
            out = lax.dot_general(left, right, tn, preferred_element_type=f32) * scale
            gpart[b, g, cut, :, :, pl.ds(col, chunk)] = out.astype(bf).reshape(groups, rows, chunk)

    def bucket(b, g, h, chip, core):
        dev = 2 * chip + core
        return gpart.at[b, g, lax.rem(dev, cuts), dev // cuts, :, pl.ds(h * sub, sub)]

    def number(b, g, h):
        return (2 * b + g) * parts + h

    def rs_pal(b, g, h, chip, core):
        q = number(b, g, h)
        return remote(
            bucket(b, g, h, chip, core), sibl.at[q, chip],
            rsib_send.at[q, chip], rsib_recv.at[q, chip], {"dp": pal},
        )

    def rs_hop(side, b, g, h, k, dest):
        q = number(b, g, h)
        to = d + 2 if side == 0 else d - 2
        return remote(
            bucket(b, g, h, dest, c), rland.at[side, q, k - 1],
            rs_send.at[side, q, k - 1], rs_recv.at[side, q, k - 1], {"dp": to},
        )

    def add_into(target, *others):
        for at in range(0, sub, strip):
            value = target[:, pl.ds(at, strip)].astype(f32)
            for other in others:
                value = value + other[:, pl.ds(at, strip)].astype(f32)
            target[:, pl.ds(at, strip)] = value.astype(bf)

    def nth(n):
        return jnp.where(2 * z < chips, last - n, n)

    def rs_exchange(b, g):
        for h in range(parts):
            steps(0, chips, lambda n: rs_pal(b, g, h, nth(n), 1 - c).start())

    def rs_start(b, g, h):
        def one(n):
            chip = nth(n)
            rs_pal(b, g, h, chip, c).wait_recv()
            add_into(bucket(b, g, h, chip, c), sibl.at[number(b, g, h), chip])

            @pl.when((z == 0) & (n < last))
            def _():
                rs_hop(0, b, g, h, n + 1, chip).start()

            @pl.when((z == last) & (n < last))
            def _():
                rs_hop(1, b, g, h, n + 1, chip).start()

        steps(0, chips, one)

    def rs_service(b, g, h):
        q = number(b, g, h)

        def one(k):
            @pl.when((z >= 1) & (k >= z))
            def _():
                dest = chips - k + z - 1
                rs_hop(0, b, g, h, k, dest).wait_recv()
                add_into(bucket(b, g, h, dest, c), rland.at[0, q, k - 1])
                rs_hop(0, b, g, h, k + 1, dest).start()

            @pl.when((z < last) & (k >= last - z))
            def _():
                dest = z + k - last
                rs_hop(1, b, g, h, k, dest).wait_recv()
                add_into(bucket(b, g, h, dest, c), rland.at[1, q, k - 1])
                rs_hop(1, b, g, h, k + 1, dest).start()

        steps(1, last, one)

    def rs_finish(b, g, h):
        q = number(b, g, h)

        @pl.when(z >= 1)
        def _():
            rs_hop(0, b, g, h, last, z).wait_recv()

        @pl.when(z < last)
        def _():
            rs_hop(1, b, g, h, last, z).wait_recv()

        own = bucket(b, g, h, z, c)

        def put(*others):
            for at in range(0, sub, strip):
                value = own[:, pl.ds(at, strip)].astype(f32)
                for other in others:
                    value = value + other[:, pl.ds(at, strip)].astype(f32)
                reduced[b, g, :, pl.ds(h * sub + at, strip)] = value.astype(bf)

        @pl.when(z == 0)
        def _():
            put(rland.at[1, q, last - 1])

        @pl.when(z == last)
        def _():
            put(rland.at[0, q, last - 1])

        @pl.when((z > 0) & (z < last))
        def _():
            put(rland.at[0, q, last - 1], rland.at[1, q, last - 1])

    def rs_drain(b, g, h):
        steps(0, chips, lambda chip: rs_pal(b, g, h, chip, 1 - c).wait_send())

        def one(k):
            @pl.when(k >= z + 1)
            def _():
                rs_hop(0, b, g, h, k, chips - k + z).wait_send()

            @pl.when(k >= chips - z)
            def _():
                rs_hop(1, b, g, h, k, k - chips + z).wait_send()

        steps(1, chips, one)

    def sec_hop(b, g, h, k, owner):
        q = number(b, g, h)
        at = pl.ds(h * sub, sub)
        return remote(
            reduced.at[b, g, :, at], every.at[owner, b, g, :, at],
            sec_send.at[q, k - 1], sec_recv.at[q, k - 1],
            {"section": lax.rem(me + k, sections)},
        )

    def own_put(b, g, h):
        at = pl.ds(h * sub, sub)
        return pltpu.make_async_copy(
            reduced.at[b, g, :, at], every.at[me, b, g, :, at], put_sem.at[number(b, g, h)]
        )

    def sec_start(b, g, h):
        for k in range(1, sections):
            sec_hop(b, g, h, k, me).start()
        own_put(b, g, h).start()

    def sec_drain(b, g, h):
        for k in range(1, sections):
            sec_hop(b, g, h, k, lax.rem(me + sections - k, sections)).wait_recv()
        for k in range(1, sections):
            sec_hop(b, g, h, k, me).wait_send()
        own_put(b, g, h).wait()

    def contract(b, g, h):
        out = jnp.zeros((combos, cond_width), f32)
        for p in range(per):
            for at in range(h * sub, (h + 1) * sub, strip):
                out += lax.dot_general(
                    reduced[b, g, p * combos : (p + 1) * combos, pl.ds(at, strip)],
                    gens[g, :, pl.ds(p * piece + at, strip)], nt, preferred_element_type=f32,
                )
        part[b] += out

    def slot_hop(k, owner):
        ref = slots_all.at[owner]
        return remote(
            slots_own, ref, slot_send.at[k - 1], slot_recv.at[k - 1],
            {"section": lax.rem(me + k, sections)},
        )

    def sum_hop(k):
        return remote(
            sums.at[d], sums.at[d], sum_send.at[k - 1], sum_recv.at[d],
            {"dp": lax.rem(d + k, ways)},
        )

    def task_hop(k, owner):
        return remote(
            task_out.at[owner], task_out.at[owner], task_send.at[k - 1], task_recv.at[k - 1],
            {"section": lax.rem(me + k, sections)},
        )

    top = blocks - 1
    pieces = [(g, h) for g in (0, 1) for h in range(parts)]
    generate(0)
    pl.semaphore_wait(barrier, ways - 1 + sections - 1)
    ag_start(top, 0)
    generate(1)
    ag_start(top, 1)
    for k in range(1, sections):
        slot_hop(k, me).start()
    weigh()
    part[...] = jnp.zeros_like(part)
    hid_copy.wait()
    norm(top)

    def both(fn, b, k):
        for g in (0, 1):
            fn(b, g, k)

    steps(1, last, lambda k: both(ag_service, top, k))
    if top > 0:
        for g in (0, 1):
            ag_start(top - 1, g)
    for b in reversed(range(top)):
        norm(b)
    for k in range(1, sections):
        slot_hop(k, lax.rem(me + sections - k, sections)).wait_recv()
    slots_all[me] = slots_own[...]
    pre_all = task[...][None, None, :, None, :] + slots_all[...][:, :, None, :, :]
    cond_all[...] = (
        (pre_all / (1.0 + jnp.exp(-pre_all))).reshape(sections * blocks * combos, cond_width).astype(bf)
    )
    ag_service(top, 0, last)
    ag_finish(top, 0)
    project(top)
    ag_service(top, 1, last)
    ag_finish(top, 1)

    @pl.when(me == sections - 1)
    def _():
        pltpu.make_async_copy(grad_in, landed.at[pl.ds(0, micro)], in_sem.at[1]).wait()

    early = me < sections // 2
    for b in reversed(range(blocks)):
        ready, later = [], pieces
        if b < top:
            ready, later = pieces[:parts], pieces[parts:]

            @pl.when(early)
            def _():
                for g, h in ready:
                    rs_service(b + 1, g, h)

        if b > 0 and last > 1:
            @pl.when(early)
            def _():
                both(ag_service, b - 1, 1)

        def between(m):
            if b > 0 and last > 1:
                @pl.when(jnp.logical_not(early) & (m == micro // 2))
                def _():
                    ag_service(b - 1, 0, 1)

            if b < top:
                @pl.when(early & (m == micro // 2))
                def _():
                    rs_service(b + 1, *later[0])

        relay(b, between)
        if b > 0:
            if last > 1:
                @pl.when(jnp.logical_not(early))
                def _():
                    ag_service(b - 1, 1, 1)

        if b < top:
            @pl.when(jnp.logical_not(early))
            def _():
                for g, h in ready + later[:1]:
                    rs_service(b + 1, g, h)

            for g, h in later[1:]:
                rs_service(b + 1, g, h)
        for g in (0, 1):
            grads(b, g)
            if b == 0:
                rs_exchange(b, g)
        if b > 0:
            steps(2, last, lambda k: both(ag_service, b - 1, k))
            for g in (0, 1):
                rs_exchange(b, g)
            for g, h in pieces:
                rs_start(b, g, h)
            ag_service(b - 1, 0, last)
            ag_finish(b - 1, 0)
            project(b - 1)
            ag_service(b - 1, 1, last)
            ag_finish(b - 1, 1)
            if b - 1 > 0:
                for g in (0, 1):
                    ag_start(b - 2, g)
        else:
            for g, h in pieces:
                rs_start(b, g, h)
        if b < top:
            for g, h in pieces:
                rs_finish(b + 1, g, h)
                sec_start(b + 1, g, h)
            for g, h in pieces:
                contract(b + 1, g, h)
    for g, h in pieces:
        rs_service(0, g, h)
        rs_finish(0, g, h)
        sec_start(0, g, h)
        contract(0, g, h)

    d_pre = part[...].reshape(blocks, tasks, experts, cond_width) * sig * (1.0 + pre * (1.0 - sig))
    slot_rows = blocks * experts
    sums[d] = jnp.zeros_like(sums[d])
    sums[d, pl.ds(0, slot_rows)] = jnp.sum(d_pre, axis=1).reshape(slot_rows, cond_width)
    sums[d, pl.ds(slot_rows, tasks)] = jnp.sum(d_pre, axis=(0, 2))
    steps(1, ways, lambda k: sum_hop(k).start())

    def sum_wait(k):
        other = lax.rem(d + k, ways)
        remote(
            sums.at[other], sums.at[other], sum_send.at[k - 1], sum_recv.at[other], {"dp": other}
        ).wait_recv()

    steps(1, ways, sum_wait)
    whole = jnp.sum(sums[...], axis=0)
    slot_out[...] = whole[:slot_rows]
    task_out[me] = whole[slot_rows:]
    for k in range(1, sections):
        task_hop(k, me).start()

    for b in range(blocks):
        for g in (0, 1):
            ag_drain(b, g)
        for g, h in pieces:
            rs_drain(b, g, h)
    steps(0, total, relay_drain)
    steps(0, micro, lambda m: hid_put(m).wait())
    steps(1, ways, lambda k: sum_hop(k).wait_send())
    for k in range(1, sections):
        slot_hop(k, me).wait_send()
        task_hop(k, lax.rem(me + sections - k, sections)).wait_recv()
        task_hop(k, me).wait_send()
    for b in range(blocks):
        for g, h in pieces:
            sec_drain(b, g, h)


def generators(
    cond, every, hid, slot_sum, task_sums, hid_out, down, up, task_out, slot_out
):
    rows = cond.shape[0]
    for g, out in ((0, down), (1, up)):
        right = every[:, :, g].reshape(rows, every.shape[-1])
        out[...] = lax.dot_general(cond[...], right, tn, preferred_element_type=f32)
    hid_out[...] = hid[...]
    slot_out[...] = slot_sum[...]
    task_out[...] = jnp.sum(task_sums[...], axis=0)[: task_out.shape[0]]


def on_device(
    hidden_in, out_grad, gate_probs, expert_ids, task_ids, task_embed, slot_embed, gen_down, gen_up
):
    sections, ways = lax.axis_size("section"), lax.axis_size("dp")
    blocks, _, micro, tok, width = hidden_in.shape
    tasks, cond_width = task_embed.shape
    experts = slot_embed.shape[2]
    combos = tasks * experts
    span = gen_down.shape[1]
    per = max(1, span // width)
    cuts = max(1, width // span)
    piece = span // per
    rows = per * combos
    groups = ways // cuts
    ranks = groups * rows
    total, tokens, chips = blocks * micro, micro * tok, ways // 2
    quads = 2 * blocks
    chunk = min(piece, 1024)

    slots_own = slot_embed[:, 0]
    gates = gate_probs[:, 0].transpose(0, 1, 3, 2)
    picks = expert_ids[:, 0].transpose(0, 1, 3, 2)
    parts = 2
    sub = piece // parts

    vmem = pl.BlockSpec(memory_space=pltpu.VMEM)
    anywhere = pl.BlockSpec(memory_space=pl.ANY)
    sem = pltpu.SemaphoreType.DMA
    sizes = (sections, ways, blocks, micro, tok, width, tasks, experts, per, cuts, piece)
    hidden, every, cond_all, slot_sum, task_sums = pl.pallas_call(
        functools.partial(backward, sizes),
        out_shape=(
            jax.ShapeDtypeStruct((micro, tok, width), bf),
            jax.ShapeDtypeStruct((sections, blocks, 2, rows, piece), bf),
            jax.ShapeDtypeStruct((sections * blocks * combos, cond_width), bf),
            jax.ShapeDtypeStruct((blocks * experts, cond_width), f32),
            jax.ShapeDtypeStruct((sections, 8, cond_width), f32),
        ),
        in_specs=[
            anywhere, anywhere, vmem, vmem, pl.BlockSpec(memory_space=pltpu.SMEM), vmem, vmem,
            anywhere, anywhere,
        ],
        out_specs=(anywhere, anywhere, vmem, vmem, vmem),
        scratch_shapes=[
            pltpu.VMEM((2, cond_width, span), bf),
            pltpu.VMEM((blocks, tokens, width), bf),
            pltpu.VMEM((blocks, tokens, width), bf),
            pltpu.VMEM((blocks, tokens, 1), f32),
            pltpu.VMEM((blocks, tokens, ranks), f32),
            pltpu.VMEM((blocks, tokens, ranks), bf),
            pltpu.VMEM((blocks, tokens, ranks), bf),
            pltpu.VMEM((total, tok, width), bf),
            pltpu.VMEM((total, tok, width), bf),
            pltpu.VMEM((blocks, 2, cuts, groups, rows, piece), bf),
            pltpu.VMEM((blocks, 2, cuts, groups, rows, piece), bf),
            pltpu.VMEM((quads * parts, chips, rows, sub), bf),
            pltpu.VMEM((2, quads * parts, chips - 1, rows, sub), bf),
            pltpu.VMEM((blocks, tokens, ranks), f32),
            pltpu.VMEM((blocks, 2, rows, piece), bf),
            pltpu.VMEM((sections, blocks, experts, cond_width), f32),
            pltpu.VMEM((blocks, combos, cond_width), f32),
            pltpu.VMEM((ways, blocks * experts + 8, cond_width), f32),
            sem((2, span // chunk)),
            sem((2,)),
            sem((micro,)),
            sem((quads * parts,)),
            sem((2, quads, chips - 1)),
            sem((2, quads, chips - 1)),
            sem((quads, chips)),
            sem((quads, chips)),
            sem((quads * parts, chips)),
            sem((quads * parts, chips)),
            sem((2, quads * parts, chips - 1)),
            sem((2, quads * parts, chips - 1)),
            sem((quads * parts, sections - 1)),
            sem((quads * parts, sections - 1)),
            sem((total, 4)),
            sem((total, 4)),
            sem((sections - 1,)),
            sem((sections - 1,)),
            sem((ways - 1,)),
            sem((ways,)),
            sem((sections - 1,)),
            sem((sections - 1,)),
        ],
        compiler_params=pltpu.CompilerParams(
            collective_id=1, has_side_effects=True, vmem_limit_bytes=58 << 20
        ),
        name="backward",
    )(
        hidden_in.reshape(blocks, tokens, width), out_grad, gates, picks, task_ids, slots_own,
        task_embed, gen_down, gen_up,
    )

    out_chunk = min(piece, 1024)
    across = piece // out_chunk
    strip = width // (per * across)
    here = pl.BlockSpec((tokens, strip), lambda p, i: (0, p * across + i))
    columns = pl.BlockSpec((cond_width, out_chunk), lambda p, i: (0, p * across + i))

    def fixed(*shape):
        return pl.BlockSpec(shape, lambda p, i: (0,) * len(shape))

    d_hidden, d_down, d_up, d_task, d_slot = pl.pallas_call(
        generators,
        grid=(per, across),
        out_shape=(
            jax.ShapeDtypeStruct((tokens, width), bf),
            jax.ShapeDtypeStruct((cond_width, span), f32),
            jax.ShapeDtypeStruct((cond_width, span), f32),
            jax.ShapeDtypeStruct((tasks, cond_width), f32),
            jax.ShapeDtypeStruct((blocks * experts, cond_width), f32),
        ),
        in_specs=[
            fixed(sections * blocks * combos, cond_width),
            pl.BlockSpec((sections, blocks, 2, combos, out_chunk), lambda p, i: (0, 0, 0, p, i)),
            here,
            fixed(blocks * experts, cond_width),
            fixed(sections, 8, cond_width),
        ],
        out_specs=(
            here, columns, columns, fixed(tasks, cond_width), fixed(blocks * experts, cond_width)
        ),
        compiler_params=pltpu.CompilerParams(vmem_limit_bytes=58 << 20),
        name="generators",
    )(cond_all, every, hidden.reshape(tokens, width), slot_sum, task_sums)
    return (
        d_hidden.reshape(1, micro, tok, width), d_down, d_up, d_task,
        d_slot.reshape(blocks, 1, experts, cond_width),
    )


def solution(mesh):
    placed = (
        P(None, "section", None, "dp", None),
        P(None, "dp", None),
        P(None, "section", None, "dp", None),
        P(None, "section", None, "dp", None),
        P(None, "dp"),
        P(),
        P(None, "section", None, None),
        P(None, "dp"),
        P(None, "dp"),
    )
    return jax.shard_map(
        on_device,
        mesh=mesh,
        in_specs=placed,
        out_specs=(
            P("section", None, "dp", None),
            P(None, "dp"),
            P(None, "dp"),
            P(),
            P(None, "section", None, None),
        ),
        check_vma=False,
    )
```

time: 200 us -> 181 us (0.905)
  Pallas kernels: 190 us -> 179 us
  local copies, waits for them, and re-layouts: 6.07 us -> 1.31 us
  other arithmetic: 2.76 us -> 0 us
    pallas_call x1, Pallas kernels: 183 us -> 169 us  [on_device(): pl.pallas_call(functools.partial(backward, sizes), out_shape=(jax.ShapeDt...]
    unnamed x13 -> x1, local copies, waits for them, and re-layouts: 5.01 us -> 1.31 us
    pallas_call x1, Pallas kernels: 7.29 us -> 9.73 us  [on_device(): pl.pallas_call(generators, grid=(per, across), out_shape=(jax.ShapeDtypeS...]
where the time goes in v2:
time: 181 us
  Pallas kernels  179 us (99%)
    pallas_call x1, Pallas kernels, on_device(): pl.pallas_call(functools.partial(backward, sizes), out_shape=(jax.ShapeDt...  169 us
    pallas_call x1, Pallas kernels, on_device(): pl.pallas_call(generators, grid=(per, across), out_shape=(jax.ShapeDtypeS...  9.73 us

profile of v2, /device:TPU:0, one launch (start us, length us, event | category | flops | bytes accessed | tf_op | source)
XLA Modules:
  0.0 181.0 jit_solution(15065382161519309907)
XLA Ops:
  0.6 1.3 copy.14.task_ids
  1.9 169.3 %backward.1 = (bf16[4,16,4096]{2,1,0:T(8,128)(2,1)}, bf16[4,2,2,32,4096]{4,3,2,1,0:T(8,128)(2,1)}, bf16[128,256]{1,0:T(8,128)(2,1)}, f32[16,256]{1,0:T(8,128)}, f32[4,8,256]{2,1,0:T(8,128)}) custom-call(bf16[2,64,4096]{2,1,0:T(8,128)(2,1)} %bitcast.13, bf16[4,16,4096]{2,1,0:T(8,128)(2,1)} %grad_in.1, f32[2,4,2,16]{3,2,1,0:T(2,128)} %bitcast.16, ...), custom_call_target="tpu_custom_call" | custom-call | tf_op jit(solution)/shard_map/backward/pallas_call | solution.py:665
  171.3 9.7 %generators.1 = (bf16[64,4096]{1,0:T(8,128)(2,1)}, f32[256,8192]{1,0:T(8,128)}, f32[256,8192]{1,0:T(8,128)}, f32[2,256]{1,0:T(2,128)}, f32[16,256]{1,0:T(8,128)}) custom-call(bf16[128,256]{1,0:T(8,128)(2,1)} %get-tuple-element.15.cond, bf16[4,2,2,32,4096]{4,3,2,1,0:T(8,128)(2,1)} %get-tuple-element.16.every, bf16[64,4096]{1,0:T(8,128)(2,1)} %bitcast.14, ...), custom_call_target="tpu_custom_call" | custom-call | tf_op jit(solution)/shard_map/generators/pallas_call | solution.py:739

commit v3 on v2

--- a/solution.py
+++ b/solution.py
@@ -39,8 +39,7 @@
     chunk = min(piece, 1024)
     hop = width // 4
     parts = rland.shape[1] // (2 * blocks)
-    sub = piece // parts
-    strip = min(sub, 1024)
+    sub = rows // parts
     tokens = micro * tok
     total = blocks * micro
     below, above = lax.rem(me + sections - 1, sections), lax.rem(me + 1, sections)
@@ -60,7 +59,7 @@
         lax.fori_loop(low, high, run, 0)
 
     gen_copies = []
-    for g, source in ((1, gen_up), (0, gen_down)):
+    for g, source in ((0, gen_down), (1, gen_up)):
         for n, at in enumerate(range(0, per * piece, chunk)):
             gen_copies.append(
                 pltpu.make_async_copy(
@@ -107,7 +106,7 @@
             return jnp.sum(jnp.where(eye, row, 0.0), axis=1, keepdims=True)
 
         for m in range(micro):
-            right_task = jnp.where(task_of == task_ids[m, 0], 1.0, 0.0)
+            right_task = jnp.where(task_of == task_ids[m], 1.0, 0.0)
             for b in range(blocks):
                 total_weight = jnp.zeros((tok, ranks), f32)
                 for k in range(gates.shape[2]):
@@ -118,7 +117,7 @@
 
     def generate(g):
         for n, at in enumerate(range(0, per * piece, chunk)):
-            gen_copies[(1 - g) * (per * piece // chunk) + n].wait()
+            gen_copies[g * (per * piece // chunk) + n].wait()
             out = jnp.dot(cond, gens[g, :, pl.ds(at, chunk)], preferred_element_type=f32).astype(bf)
             row, col = at // piece * combos, at % piece
             for b in range(blocks):
@@ -296,7 +295,7 @@
 
     def bucket(b, g, h, chip, core):
         dev = 2 * chip + core
-        return gpart.at[b, g, lax.rem(dev, cuts), dev // cuts, :, pl.ds(h * sub, sub)]
+        return gpart.at[b, g, lax.rem(dev, cuts), dev // cuts, pl.ds(h * sub, sub)]
 
     def number(b, g, h):
         return (2 * b + g) * parts + h
@@ -317,11 +316,11 @@
         )
 
     def add_into(target, *others):
-        for at in range(0, sub, strip):
-            value = target[:, pl.ds(at, strip)].astype(f32)
+        for at in range(0, piece, chunk):
+            value = target[:, pl.ds(at, chunk)].astype(f32)
             for other in others:
-                value = value + other[:, pl.ds(at, strip)].astype(f32)
-            target[:, pl.ds(at, strip)] = value.astype(bf)
+                value = value + other[:, pl.ds(at, chunk)].astype(f32)
+            target[:, pl.ds(at, chunk)] = value.astype(bf)
 
     def nth(n):
         return jnp.where(2 * z < chips, last - n, n)
@@ -346,25 +345,30 @@
 
         steps(0, chips, one)
 
-    def rs_service(b, g, h):
+    def rs_service(b, buckets, low, high):
+        def one(k):
+            for g, h in buckets:
+                rs_step(b, g, h, k)
+
+        if high > low:
+            steps(low, high, one)
+
+    def rs_step(b, g, h, k):
         q = number(b, g, h)
 
-        def one(k):
-            @pl.when((z >= 1) & (k >= z))
-            def _():
-                dest = chips - k + z - 1
-                rs_hop(0, b, g, h, k, dest).wait_recv()
-                add_into(bucket(b, g, h, dest, c), rland.at[0, q, k - 1])
-                rs_hop(0, b, g, h, k + 1, dest).start()
-
-            @pl.when((z < last) & (k >= last - z))
-            def _():
-                dest = z + k - last
-                rs_hop(1, b, g, h, k, dest).wait_recv()
-                add_into(bucket(b, g, h, dest, c), rland.at[1, q, k - 1])
-                rs_hop(1, b, g, h, k + 1, dest).start()
-
-        steps(1, last, one)
+        @pl.when((z >= 1) & (k >= z))
+        def _():
+            dest = chips - k + z - 1
+            rs_hop(0, b, g, h, k, dest).wait_recv()
+            add_into(bucket(b, g, h, dest, c), rland.at[0, q, k - 1])
+            rs_hop(0, b, g, h, k + 1, dest).start()
+
+        @pl.when((z < last) & (k >= last - z))
+        def _():
+            dest = z + k - last
+            rs_hop(1, b, g, h, k, dest).wait_recv()
+            add_into(bucket(b, g, h, dest, c), rland.at[1, q, k - 1])
+            rs_hop(1, b, g, h, k + 1, dest).start()
 
     def rs_finish(b, g, h):
         q = number(b, g, h)
@@ -380,11 +384,11 @@
         own = bucket(b, g, h, z, c)
 
         def put(*others):
-            for at in range(0, sub, strip):
-                value = own[:, pl.ds(at, strip)].astype(f32)
+            for at in range(0, piece, chunk):
+                value = own[:, pl.ds(at, chunk)].astype(f32)
                 for other in others:
-                    value = value + other[:, pl.ds(at, strip)].astype(f32)
-                reduced[b, g, :, pl.ds(h * sub + at, strip)] = value.astype(bf)
+                    value = value + other[:, pl.ds(at, chunk)].astype(f32)
+                reduced[b, g, pl.ds(h * sub, sub), pl.ds(at, chunk)] = value.astype(bf)
 
         @pl.when(z == 0)
         def _():
@@ -416,7 +420,7 @@
         q = number(b, g, h)
         at = pl.ds(h * sub, sub)
         return remote(
-            reduced.at[b, g, :, at], every.at[owner, b, g, :, at],
+            reduced.at[b, g, at], every.at[owner, b, g, at],
             sec_send.at[q, k - 1], sec_recv.at[q, k - 1],
             {"section": lax.rem(me + k, sections)},
         )
@@ -424,7 +428,7 @@
     def own_put(b, g, h):
         at = pl.ds(h * sub, sub)
         return pltpu.make_async_copy(
-            reduced.at[b, g, :, at], every.at[me, b, g, :, at], put_sem.at[number(b, g, h)]
+            reduced.at[b, g, at], every.at[me, b, g, at], put_sem.at[number(b, g, h)]
         )
 
     def sec_start(b, g, h):
@@ -441,11 +445,12 @@
 
     def contract(b, g, h):
         out = jnp.zeros((combos, cond_width), f32)
-        for p in range(per):
-            for at in range(h * sub, (h + 1) * sub, strip):
+        for row in range(h * sub, (h + 1) * sub, combos):
+            for at in range(0, piece, chunk):
                 out += lax.dot_general(
-                    reduced[b, g, p * combos : (p + 1) * combos, pl.ds(at, strip)],
-                    gens[g, :, pl.ds(p * piece + at, strip)], nt, preferred_element_type=f32,
+                    reduced[b, g, row : row + combos, pl.ds(at, chunk)],
+                    gens[g, :, pl.ds(row // combos * piece + at, chunk)], nt,
+                    preferred_element_type=f32,
                 )
         part[b] += out
 
@@ -510,15 +515,14 @@
         pltpu.make_async_copy(grad_in, landed.at[pl.ds(0, micro)], in_sem.at[1]).wait()
 
     early = me < sections // 2
+    late = jnp.logical_not(early)
+    first, rest = pieces[:parts], pieces[parts:]
+    turn, half = min(2, last), (parts + 1) // 2
     for b in reversed(range(blocks)):
-        ready, later = [], pieces
         if b < top:
-            ready, later = pieces[:parts], pieces[parts:]
-
             @pl.when(early)
             def _():
-                for g, h in ready:
-                    rs_service(b + 1, g, h)
+                rs_service(b + 1, first, 1, last)
 
         if b > 0 and last > 1:
             @pl.when(early)
@@ -527,38 +531,31 @@
 
         def between(m):
             if b > 0 and last > 1:
-                @pl.when(jnp.logical_not(early) & (m == micro // 2))
+                @pl.when(late & (m == micro // 2))
                 def _():
                     ag_service(b - 1, 0, 1)
 
             if b < top:
-                @pl.when(early & (m == micro // 2))
+                @pl.when(early & (m == micro // 4))
                 def _():
-                    rs_service(b + 1, *later[0])
+                    rs_service(b + 1, rest[:half], 1, turn)
+
+                @pl.when(early & (m == micro - 1))
+                def _():
+                    rs_service(b + 1, rest[:half], turn, last)
+                    rs_service(b + 1, rest[half:], 1, turn)
 
         relay(b, between)
         if b > 0:
             if last > 1:
-                @pl.when(jnp.logical_not(early))
+                @pl.when(late)
                 def _():
                     ag_service(b - 1, 1, 1)
 
-        if b < top:
-            @pl.when(jnp.logical_not(early))
-            def _():
-                for g, h in ready + later[:1]:
-                    rs_service(b + 1, g, h)
-
-            for g, h in later[1:]:
-                rs_service(b + 1, g, h)
-        for g in (0, 1):
-            grads(b, g)
-            if b == 0:
+            for g in (0, 1):
+                grads(b, g)
                 rs_exchange(b, g)
-        if b > 0:
-            steps(2, last, lambda k: both(ag_service, b - 1, k))
-            for g in (0, 1):
-                rs_exchange(b, g)
+                steps(2, last, lambda k: ag_service(b - 1, g, k))
             for g, h in pieces:
                 rs_start(b, g, h)
             ag_service(b - 1, 0, last)
@@ -569,20 +566,38 @@
             if b - 1 > 0:
                 for g in (0, 1):
                     ag_start(b - 2, g)
-        else:
+        if b < top:
+            @pl.when(late)
+            def _():
+                rs_service(b + 1, pieces, 1, turn)
+
+        if b == 0:
+            for g in (0, 1):
+                grads(b, g)
+                rs_exchange(b, g)
             for g, h in pieces:
                 rs_start(b, g, h)
         if b < top:
+            @pl.when(late)
+            def _():
+                rs_service(b + 1, pieces, turn, last)
+
+            @pl.when(early)
+            def _():
+                rs_service(b + 1, rest[half:], turn, last)
+
             for g, h in pieces:
                 rs_finish(b + 1, g, h)
                 sec_start(b + 1, g, h)
-            for g, h in pieces:
-                contract(b + 1, g, h)
-    for g, h in pieces:
-        rs_service(0, g, h)
-        rs_finish(0, g, h)
-        sec_start(0, g, h)
-        contract(0, g, h)
+    for n in range(len(pieces) + 1):
+        if n < len(pieces):
+            rs_service(0, pieces[n : n + 1], 1, last)
+        if n > 0:
+            g, h = pieces[n - 1]
+            rs_finish(0, g, h)
+            sec_start(0, g, h)
+            for b in range(blocks):
+                contract(b, g, h)
 
     d_pre = part[...].reshape(blocks, tasks, experts, cond_width) * sig * (1.0 + pre * (1.0 - sig))
     slot_rows = blocks * experts
@@ -655,8 +670,8 @@
     slots_own = slot_embed[:, 0]
     gates = gate_probs[:, 0].transpose(0, 1, 3, 2)
     picks = expert_ids[:, 0].transpose(0, 1, 3, 2)
-    parts = 2
-    sub = piece // parts
+    parts = per
+    sub = rows // parts
 
     vmem = pl.BlockSpec(memory_space=pltpu.VMEM)
     anywhere = pl.BlockSpec(memory_space=pl.ANY)
@@ -688,8 +703,8 @@
             pltpu.VMEM((total, tok, width), bf),
             pltpu.VMEM((blocks, 2, cuts, groups, rows, piece), bf),
             pltpu.VMEM((blocks, 2, cuts, groups, rows, piece), bf),
-            pltpu.VMEM((quads * parts, chips, rows, sub), bf),
-            pltpu.VMEM((2, quads * parts, chips - 1, rows, sub), bf),
+            pltpu.VMEM((quads * parts, chips, sub, piece), bf),
+            pltpu.VMEM((2, quads * parts, chips - 1, sub, piece), bf),
             pltpu.VMEM((blocks, tokens, ranks), f32),
             pltpu.VMEM((blocks, 2, rows, piece), bf),
             pltpu.VMEM((sections, blocks, experts, cond_width), f32),
@@ -723,7 +738,7 @@
         ),
         name="backward",
     )(
-        hidden_in.reshape(blocks, tokens, width), out_grad, gates, picks, task_ids, slots_own,
+        hidden_in.reshape(blocks, tokens, width), out_grad, gates, picks, task_ids.reshape(-1), slots_own,
         task_embed, gen_down, gen_up,
     )
 

time: 181 us -> 170 us (0.939)
  Pallas kernels: 179 us -> 169 us
    pallas_call x1, Pallas kernels: 169 us -> 159 us  [on_device(): pl.pallas_call(functools.partial(backward, sizes), out_shape=(jax.ShapeDt...]
where the time goes in v3:
time: 170 us; the launch traced here: 169 us
  Pallas kernels  169 us (99%)
    pallas_call x1, Pallas kernels, on_device(): pl.pallas_call(functools.partial(backward, sizes), out_shape=(jax.ShapeDt...  159 us
    pallas_call x1, Pallas kernels, on_device(): pl.pallas_call(generators, grid=(per, across), out_shape=(jax.ShapeDtypeS...  9.72 us

profile of v3, /device:TPU:0, one launch (start us, length us, event | category | flops | bytes accessed | tf_op | source)
XLA Modules:
  0.0 169.4 jit_solution(6730276861763257924)
XLA Ops:
  0.6 159.0 %backward.1 = (bf16[4,16,4096]{2,1,0:T(8,128)(2,1)}, bf16[4,2,2,32,4096]{4,3,2,1,0:T(8,128)(2,1)}, bf16[128,256]{1,0:T(8,128)(2,1)}, f32[16,256]{1,0:T(8,128)}, f32[4,8,256]{2,1,0:T(8,128)}) custom-call(bf16[2,64,4096]{2,1,0:T(8,128)(2,1)} %bitcast.14, bf16[4,16,4096]{2,1,0:T(8,128)(2,1)} %grad_in.1, f32[2,4,2,16]{3,2,1,0:T(2,128)} %bitcast.17, ...), custom_call_target="tpu_custom_call" | custom-call | tf_op jit(solution)/shard_map/backward/pallas_call | solution.py:680
  159.7 9.7 %generators.1 = (bf16[64,4096]{1,0:T(8,128)(2,1)}, f32[256,8192]{1,0:T(8,128)}, f32[256,8192]{1,0:T(8,128)}, f32[2,256]{1,0:T(2,128)}, f32[16,256]{1,0:T(8,128)}) custom-call(bf16[128,256]{1,0:T(8,128)(2,1)} %get-tuple-element.15.cond, bf16[4,2,2,32,4096]{4,3,2,1,0:T(8,128)(2,1)} %get-tuple-element.16.every, bf16[64,4096]{1,0:T(8,128)(2,1)} %bitcast.15, ...), custom_call_target="tpu_custom_call" | custom-call | tf_op jit(solution)/shard_map/generators/pallas_call | solution.py:754
